TPU v7x, 32 devices: a whole 2x2x4 slice. The times are simulated.
32 devices in a mesh: intra: 4 (over y, x), inter: 8 (over z, core).
Axes of the slice: x: 2, y: 2, z: 4, core: 2. Of those that a mesh axis runs over, the one named last changes fastest.
Arguments:
- acts: bfloat16 [4096, 4096], P(('intra', 'inter')), may hold values from -6 to 6
- grad_out: bfloat16 [4096, 512], P(('intra', 'inter')), may hold values from -6 to 6
- codes: int32 [4096, 512], P('intra'), may hold values from -127 to 127
- scales: float32 [2048], P('intra'), may hold values from 0.0002 to 0.0008
Outputs:
- grad_in: bfloat16 [4096, 4096], P(('intra', 'inter'))
- grad_w: float32 [4096, 512], P(('intra', 'inter'))
All inputs are finite; a program needn't handle non-finite values.
Results may differ from a plain program's by a relative error of at most 0.0049.
Values may be sent and summed in bfloat16 or wider, within the bound.
A program may use at most 64 MiB of HBM per device.

v0:
```python
import functools
import math

import jax
import jax.numpy as jnp
from jax import lax
from jax.experimental import pallas as pl
from jax.experimental.pallas import tpu as pltpu
from jax.sharding import PartitionSpec as P

MESH = pl.DeviceIdType.MESH


def flip(index, mask, extent):
    out = 0
    bit = 1
    while bit < extent:
        digit = lax.rem(index // bit, 2)
        out = out + bit * (1 - digit if mask & bit else digit)
        bit *= 2
    return out


def lane_scale(scale_row, half):
    pick = (
        lax.broadcasted_iota(jnp.int32, (half // 2, half), 1) // 2
        == lax.broadcasted_iota(jnp.int32, (half // 2, half), 0)
    ).astype(jnp.float32).astype(jnp.bfloat16)
    rest = jnp.broadcast_to(scale_row, (16, half // 2))
    total = jnp.zeros((16, half), jnp.float32)
    for _ in range(3):
        top = rest.astype(jnp.bfloat16)
        total = total + jnp.dot(top, pick, preferred_element_type=jnp.float32)
        rest = rest - top.astype(jnp.float32)
    return total[0:1]


def kernel(
    ni, nj, acts, go, codes, scales, gin, gw,
    go_all, acts_v, codes_v, scale_v, code_b, ac, pieces, part, rs,
    load_sem, go_send, go_recv, gh_send, gh_recv, fw_send, a_send, a_recv, p_send, p_recv,
    r_send, r_recv,
):
    tok, width = acts.shape
    rows = codes.shape[0]
    half = rows // 2
    nz = nj // 2
    blk = rows // nj
    i = lax.axis_index("intra")
    j = lax.axis_index("inter")
    z = j // 2
    c = lax.rem(j, 2)
    oc = 1 - c
    me = 2 * i + c
    peers = {d: flip(i, d, ni) for d in range(ni)}
    near, diag = (1, 2), 3
    cores = (c, oc)

    def dev(ii, zz, cc):
        return {"intra": ii, "inter": 2 * zz + cc}

    def rdma(src, dst, s, r, where):
        return pltpu.make_async_remote_copy(
            src_ref=src, dst_ref=dst, send_sem=s, recv_sem=r, device_id=where, device_id_type=MESH
        )

    def arrived(ref, s, r):
        rdma(ref, ref, s, r, dev(i, z, oc)).wait_recv()

    sends = []

    def send(*args):
        cp = rdma(*args)
        cp.start()
        sends.append(cp)

    def go_slot(m):
        return go_all.at[pl.ds(pl.multiple_of(m * tok, tok), tok)]

    def go_half(m, n):
        return go_all.at[pl.ds(pl.multiple_of(m * tok + n * (tok // 2), tok // 2), tok // 2)]

    def ac_slot(h, m):
        return ac.at[h, pl.ds(pl.multiple_of(m * tok, tok), tok)]

    def cols_of(ii, cc):
        return pl.ds(pl.multiple_of(ii * rows + cc * half, half), half)

    half_start = pl.multiple_of(c * half, half)
    sc_start = pl.multiple_of(c * (half // 2), half // 2)
    load_go = pltpu.make_async_copy(go, go_slot(me), load_sem.at[0])
    load_go.start()
    load_acts = pltpu.make_async_copy(acts, acts_v, load_sem.at[1])
    load_acts.start()

    load_codes = pltpu.make_async_copy(codes.at[pl.ds(half_start, half)], codes_v, load_sem.at[2])
    load_codes.start()
    load_scale = pltpu.make_async_copy(scales.at[:, pl.ds(sc_start, half // 2)], scale_v, load_sem.at[3])
    load_scale.start()
    barrier = pltpu.get_barrier_semaphore()
    count = 0
    for d in range(ni):
        for k, cc in enumerate(cores):
            if d or k:
                pl.semaphore_signal(barrier, inc=1, device_id=dev(peers[d], z, cc), device_id_type=MESH)
                count += 1
    for k in range(1, nz):
        pl.semaphore_signal(barrier, inc=1, device_id=dev(i, lax.rem(z + k, nz), c), device_id_type=MESH)
        count += 1

    load_go.wait()
    pl.semaphore_wait(barrier, count)

    for d in near:
        send(go_slot(me), go_slot(me), go_send.at[d], go_recv.at[me], dev(peers[d], z, c))
    send(go_slot(me), go_slot(me), go_send.at[0], go_recv.at[me], dev(i, z, oc))

    load_acts.wait()
    order = [lax.rem(z + k, nz) for k in range(1, nz)] + [z]
    own = []

    def send_columns(h):
        for d in near + (0, diag):
            for k, cc in enumerate(cores):
                ii = peers[d]
                col = pl.multiple_of(ii * rows + (2 * h + cc) * blk, blk)
                src = acts_v.at[:, pl.ds(col, blk)]
                if d or k:
                    m = 2 * ii + cc
                    send(src, ac_slot(h, me), a_send.at[m, h], a_recv.at[me, h], dev(ii, z, cc))
                else:
                    cp = pltpu.make_async_copy(src, ac_slot(h, me), a_recv.at[me, h])
                    cp.start()
                    own.append(cp)

    send_columns(order[0])
    load_codes.wait()
    code_b[...] = codes_v[...].astype(jnp.float32).astype(jnp.bfloat16)
    load_scale.wait()
    row_scale = lane_scale(scale_v[...], half)

    def wait_go(m):
        arrived(go_slot(m), go_send.at[0], go_recv.at[m])

    for n, d in enumerate(near):
        m = 2 * peers[d] + c
        wait_go(m)
        send(go_half(m, n), go_half(m, n), gh_send.at[n], gh_recv.at[n], dev(peers[diag ^ d], z, c))
        send(go_slot(m), go_slot(m), fw_send.at[d], go_recv.at[m], dev(i, z, oc))
    for h in order[1:]:
        send_columns(h)

    def pieces_of(ii, code, scale):
        pair = go_all[pl.ds(pl.multiple_of(2 * ii * tok, 2 * tok), 2 * tok)]
        out = lax.dot_general(
            pair, code[...], (((1,), (1,)), ((), ())), preferred_element_type=jnp.float32
        )
        return (out * scale).astype(jnp.bfloat16)

    def piece(n, cc):
        return pieces.at[n, pl.ds(pl.multiple_of(cc * tok, tok), tok)]

    for d in near:
        ii = peers[d]
        wait_go(2 * ii + oc)
        pieces[d] = pieces_of(ii, code_b, row_scale)
        for cc in cores:
            m = 2 * ii + cc
            send(piece(d, cc), gin.at[:, cols_of(i, c)], p_send.at[m], p_recv.at[me], dev(ii, z, cc))
    wait_go(2 * i + oc)
    pieces[0] = pieces_of(i, code_b, row_scale)
    send(piece(0, oc), gin.at[:, cols_of(i, c)], p_send.at[2 * i + oc], p_recv.at[me], dev(i, z, oc))
    keep = pltpu.make_async_copy(piece(0, c), gin.at[:, cols_of(i, c)], p_recv.at[me])
    keep.start()

    m = 2 * peers[diag] + c
    for n in range(2):
        arrived(go_half(m, n), gh_send.at[n], gh_recv.at[n])
    send(go_slot(m), go_slot(m), fw_send.at[diag], go_recv.at[m], dev(i, z, oc))
    wait_go(2 * peers[diag] + oc)
    dd = peers[diag]
    pieces[diag] = pieces_of(dd, code_b, row_scale)
    for cc in cores:
        m = 2 * dd + cc
        send(piece(diag, cc), gin.at[:, cols_of(i, c)], p_send.at[m], p_recv.at[me], dev(dd, z, cc))

    mine = None
    for n, h in enumerate(order):
        own[n].wait()
        for d in range(ni):
            for k, cc in enumerate(cores):
                if d or k:
                    m = 2 * peers[d] + cc
                    arrived(ac_slot(h, m), a_send.at[m, h], a_recv.at[m, h])
        term = lax.dot_general(
            ac[h], go_all[...], (((0,), (0,)), ((), ())), preferred_element_type=jnp.float32
        )
        if n < nz - 1:
            part[n] = term.astype(jnp.bfloat16)
            send(part.at[n], rs.at[z], r_send.at[n], r_recv.at[z], dev(i, h, c))
        else:
            mine = term

    for k in range(1, nz):
        h = lax.rem(z + k, nz)
        arrived(rs.at[h], r_send.at[0], r_recv.at[h])
        mine = mine + rs[h].astype(jnp.float32)
    gw[...] = mine * (1.0 / math.sqrt(tok * ni * nj))

    keep.wait()
    for d in range(ni):
        for k, cc in enumerate(cores):
            if d or k:
                ii = peers[d]
                block = gin.at[:, cols_of(ii, cc)]
                arrived(block, p_send.at[2 * ii + cc], p_recv.at[2 * ii + cc])
    for cp in sends:
        cp.wait_send()


def fused(ni, nj, acts, grad_out, codes, scales):
    tok, width = acts.shape
    kv = grad_out.shape[1]
    rows = codes.shape[0]
    half, nz, blk = rows // 2, nj // 2, rows // nj
    group = 2 * ni
    dma = pltpu.SemaphoreType.DMA
    bf16 = jnp.bfloat16
    anyspace = pl.BlockSpec(memory_space=pl.ANY)
    return tuple(pl.pallas_call(
        functools.partial(kernel, ni, nj),
        out_shape=(
            pltpu.VMEM((tok, width), bf16),
            pltpu.VMEM((blk, kv), jnp.float32),
        ),
        in_specs=[anyspace] * 4,
        out_specs=(pl.BlockSpec(memory_space=pltpu.VMEM),) * 2,
        scratch_shapes=[
            pltpu.VMEM((group * tok, kv), bf16),
            pltpu.VMEM((tok, width), bf16),
            pltpu.VMEM((half, kv), jnp.int32),
            pltpu.VMEM((1, half // 2), jnp.float32),
            pltpu.VMEM((half, kv), bf16),
            pltpu.VMEM((nz, group * tok, blk), bf16),
            pltpu.VMEM((ni, 2 * tok, half), bf16),
            pltpu.VMEM((max(nz - 1, 1), blk, kv), bf16),
            pltpu.VMEM((nz, blk, kv), bf16),
            dma((4,)),
            dma((ni,)), dma((group,)), dma((2,)), dma((2,)), dma((ni,)),
            dma((group, nz)), dma((group, nz)),
            dma((group,)), dma((group,)),
            dma((nz,)), dma((nz,)),
        ],
        compiler_params=pltpu.CompilerParams(collective_id=0, has_side_effects=True),
    )(acts, grad_out, codes, scales.reshape(1, -1)))


def plain(acts, grad_out, codes, scales):
    rows = codes.shape[0]
    width_kv = codes.shape[1]
    blocks = codes.astype(jnp.float32).reshape(rows // 2, 2 * width_kv) * scales[:, None]
    local_weight = blocks.reshape(rows, width_kv).astype(jnp.bfloat16)
    n_group = lax.axis_size("intra")
    n_cross = lax.axis_size("inter")
    factor = 1.0 / math.sqrt(acts.shape[0] * n_group * n_cross)
    contract = (((0,), (0,)), ((), ()))
    group_cot = lax.all_gather(grad_out, "intra", axis=0, tiled=True)
    columns_owned = lax.all_to_all(acts, "intra", split_axis=1, concat_axis=0, tiled=True)
    grad_w = lax.psum_scatter(
        lax.dot_general(columns_owned, group_cot, contract, preferred_element_type=jnp.float32)
        * factor,
        "inter",
        scatter_dimension=0,
        tiled=True,
    )
    pieces = jnp.dot(group_cot, local_weight.T, preferred_element_type=jnp.float32).astype(
        jnp.bfloat16
    )
    grad_in = lax.all_to_all(pieces, "intra", split_axis=0, concat_axis=1, tiled=True)
    return (grad_in, grad_w)


def solution(mesh):
    ni, nj = mesh.shape["intra"], mesh.shape["inter"]

    def per_device(acts, grad_out, codes, scales):
        rows = codes.shape[0]
        aligned = rows % (nj * 128) == 0 and rows % 512 == 0 and acts.shape[0] % 16 == 0
        if aligned and nj % 2 == 0 and ni == 4 and acts.shape[1] == ni * rows:
            return fused(ni, nj, acts, grad_out, codes, scales)
        return plain(acts, grad_out, codes, scales)

    in_specs = (
        P(("intra", "inter"), None),
        P(("intra", "inter"), None),
        P("intra", None),
        P("intra"),
    )
    out_specs = (P(("intra", "inter"), None), P(("intra", "inter"), None))
    return jax.shard_map(
        per_device, mesh=mesh, in_specs=in_specs, out_specs=out_specs, check_vma=False
    )
```

profile of v0, /device:TPU:0, one launch (start us, length us, event | category | flops | bytes accessed | tf_op | source)
XLA Modules:
  0.0 37.0 jit_solution(17246262183885056466)
XLA Ops:
  0.6 34.7 %shard_map.59 = (bf16[128,4096]{1,0:T(8,128)(2,1)S(1)}, f32[128,512]{1,0:T(8,128)S(1)}) custom-call(bf16[128,4096]{1,0:T(8,128)(2,1)} %acts.1, bf16[128,512]{1,0:T(8,128)(2,1)} %go.1, s32[1024,512]{1,0:T(8,128)} %codes.1, f32[1,512]{1,0:T(1,128)} %bitcast.1), custom_call_target="tpu_custom_call" | custom-call | tf_op jit(solution)/shard_map/pallas_call | solution.py:230
  35.3 1.0 %copy.8 = bf16[128,4096]{1,0:T(8,128)(2,1)} copy(bf16[128,4096]{1,0:T(8,128)(2,1)S(1)} %get-tuple-element.2) | data formatting | bytes 2097152
  36.3 0.7 %copy.9 = f32[128,512]{1,0:T(8,128)} copy(f32[128,512]{1,0:T(8,128)S(1)} %get-tuple-element.3) | data formatting | bytes 524288
where the time goes:
time: 37.6 us; the launch traced here: 37 us
  Pallas kernels  34.7 us (92%)
  local copies, waits for them, and re-layouts  1.67 us (4%)
  between operations  0.64 us (2%)
    pallas_call x1, Pallas kernels, fused(): pl.pallas_call(functools.partial(kernel, ni, nj), out_shape=(pltpu.VMEM((...  34.7 us
    unnamed x2, local copies, waits for them, and re-layouts  1.67 us

commit v1 on v0

--- a/solution.py
+++ b/solution.py
@@ -37,9 +37,9 @@
 
 def kernel(
     ni, nj, acts, go, codes, scales, gin, gw,
-    go_all, acts_v, codes_v, scale_v, code_b, ac, pieces, part, rs,
+    go_all, acts_v, codes_v, scale_v, code_b, code_d, scale_d, ac, pieces, part, rs,
     load_sem, go_send, go_recv, gh_send, gh_recv, fw_send, a_send, a_recv, p_send, p_recv,
-    r_send, r_recv,
+    r_send, r_recv, w_send, w_recv, s_send, s_recv, plane_sem, line_sem,
 ):
     tok, width = acts.shape
     rows = codes.shape[0]
@@ -54,6 +54,7 @@
     me = 2 * i + c
     peers = {d: flip(i, d, ni) for d in range(ni)}
     near, diag = (1, 2), 3
+    dd = peers[diag]
     cores = (c, oc)
 
     def dev(ii, zz, cc):
@@ -86,34 +87,51 @@
     def cols_of(ii, cc):
         return pl.ds(pl.multiple_of(ii * rows + cc * half, half), half)
 
+    def quarter(h):
+        return pl.ds(pl.multiple_of(h * blk, blk), blk)
+
     half_start = pl.multiple_of(c * half, half)
     sc_start = pl.multiple_of(c * (half // 2), half // 2)
+    barrier = pltpu.get_barrier_semaphore()
+    for d in range(1, ni):
+        pl.semaphore_signal(barrier, inc=1, device_id=dev(peers[d], z, 0), device_id_type=MESH)
+
+    @pl.when(c == 1)
+    def _():
+        pl.semaphore_signal(barrier, inc=1, device_id=dev(i, z, 0), device_id_type=MESH)
+
     load_go = pltpu.make_async_copy(go, go_slot(me), load_sem.at[0])
     load_go.start()
+    load_codes = pltpu.make_async_copy(codes.at[pl.ds(half_start, half)], codes_v, load_sem.at[2])
+    load_codes.start()
     load_acts = pltpu.make_async_copy(acts, acts_v, load_sem.at[1])
     load_acts.start()
-
-    load_codes = pltpu.make_async_copy(codes.at[pl.ds(half_start, half)], codes_v, load_sem.at[2])
-    load_codes.start()
     load_scale = pltpu.make_async_copy(scales.at[:, pl.ds(sc_start, half // 2)], scale_v, load_sem.at[3])
     load_scale.start()
-    barrier = pltpu.get_barrier_semaphore()
-    count = 0
-    for d in range(ni):
-        for k, cc in enumerate(cores):
-            if d or k:
-                pl.semaphore_signal(barrier, inc=1, device_id=dev(peers[d], z, cc), device_id_type=MESH)
-                count += 1
     for k in range(1, nz):
-        pl.semaphore_signal(barrier, inc=1, device_id=dev(i, lax.rem(z + k, nz), c), device_id_type=MESH)
-        count += 1
+        pl.semaphore_signal(barrier, inc=1, device_id=dev(i, lax.rem(z + k, nz), 1), device_id_type=MESH)
 
     load_go.wait()
-    pl.semaphore_wait(barrier, count)
+
+    @pl.when(c == 0)
+    def _():
+        pl.semaphore_wait(barrier, 2 * ni - 1)
+        pl.semaphore_signal(plane_sem, inc=1, device_id=dev(i, z, 1), device_id_type=MESH)
+
+    @pl.when(c == 1)
+    def _():
+        pl.semaphore_wait(plane_sem, 1)
 
     for d in near:
         send(go_slot(me), go_slot(me), go_send.at[d], go_recv.at[me], dev(peers[d], z, c))
     send(go_slot(me), go_slot(me), go_send.at[0], go_recv.at[me], dev(i, z, oc))
+
+    load_codes.wait()
+    code_b[...] = codes_v[...].astype(jnp.float32).astype(jnp.bfloat16)
+    load_scale.wait()
+    send(scale_v, scale_d, s_send, s_recv, dev(dd, z, c))
+    row_scale = lane_scale(scale_v[...], half)
+    send(code_b.at[quarter(z)], code_d.at[quarter(z)], w_send.at[0], w_recv.at[z], dev(dd, z, c))
 
     load_acts.wait()
     order = [lax.rem(z + k, nz) for k in range(1, nz)] + [z]
@@ -134,10 +152,6 @@
                     own.append(cp)
 
     send_columns(order[0])
-    load_codes.wait()
-    code_b[...] = codes_v[...].astype(jnp.float32).astype(jnp.bfloat16)
-    load_scale.wait()
-    row_scale = lane_scale(scale_v[...], half)
 
     def wait_go(m):
         arrived(go_slot(m), go_send.at[0], go_recv.at[m])
@@ -173,16 +187,27 @@
     keep = pltpu.make_async_copy(piece(0, c), gin.at[:, cols_of(i, c)], p_recv.at[me])
     keep.start()
 
-    m = 2 * peers[diag] + c
+    @pl.when(c == 1)
+    def _():
+        pl.semaphore_wait(barrier, 2 * (nz - 1))
+        pl.semaphore_signal(line_sem, inc=1, device_id=dev(i, z, 0), device_id_type=MESH)
+
+    @pl.when(c == 0)
+    def _():
+        pl.semaphore_wait(line_sem, 1)
+
+    arrived(code_d.at[quarter(z)], w_send.at[0], w_recv.at[z])
+    for k in range(1, nz):
+        send(code_d.at[quarter(z)], code_d.at[quarter(z)], w_send.at[k], w_recv.at[z],
+             dev(i, lax.rem(z + k, nz), c))
+
+    m = 2 * dd + c
     for n in range(2):
         arrived(go_half(m, n), gh_send.at[n], gh_recv.at[n])
     send(go_slot(m), go_slot(m), fw_send.at[diag], go_recv.at[m], dev(i, z, oc))
-    wait_go(2 * peers[diag] + oc)
-    dd = peers[diag]
-    pieces[diag] = pieces_of(dd, code_b, row_scale)
-    for cc in cores:
-        m = 2 * dd + cc
-        send(piece(diag, cc), gin.at[:, cols_of(i, c)], p_send.at[m], p_recv.at[me], dev(dd, z, cc))
+    arrived(scale_d, s_send, s_recv)
+    far_scale = lane_scale(scale_d[...], half)
+    wait_go(2 * dd + oc)
 
     mine = None
     for n, h in enumerate(order):
@@ -203,19 +228,41 @@
 
     for k in range(1, nz):
         h = lax.rem(z + k, nz)
+        arrived(code_d.at[quarter(h)], w_send.at[k], w_recv.at[h])
+    pieces[diag] = pieces_of(i, code_d, far_scale)
+    far = gin.at[:, cols_of(dd, c)]
+    send(piece(diag, oc), far, p_send.at[2 * dd + c], p_recv.at[2 * dd + c], dev(i, z, oc))
+    keep_far = pltpu.make_async_copy(piece(diag, c), far, load_sem.at[0])
+    keep_far.start()
+
+    for k in range(1, nz):
+        h = lax.rem(z + k, nz)
         arrived(rs.at[h], r_send.at[0], r_recv.at[h])
         mine = mine + rs[h].astype(jnp.float32)
     gw[...] = mine * (1.0 / math.sqrt(tok * ni * nj))
 
     keep.wait()
-    for d in range(ni):
+    keep_far.wait()
+    for d in (0,) + near:
         for k, cc in enumerate(cores):
             if d or k:
                 ii = peers[d]
                 block = gin.at[:, cols_of(ii, cc)]
                 arrived(block, p_send.at[2 * ii + cc], p_recv.at[2 * ii + cc])
+    arrived(gin.at[:, cols_of(dd, oc)], p_send.at[2 * dd + oc], p_recv.at[2 * dd + oc])
     for cp in sends:
         cp.wait_send()
+
+
+def leave(gin, gw, gin_out, gw_out, sem):
+    copies = [
+        pltpu.make_async_copy(gin, gin_out, sem.at[0]),
+        pltpu.make_async_copy(gw, gw_out, sem.at[1]),
+    ]
+    for cp in copies:
+        cp.start()
+    for cp in copies:
+        cp.wait()
 
 
 def fused(ni, nj, acts, grad_out, codes, scales):
@@ -227,7 +274,7 @@
     dma = pltpu.SemaphoreType.DMA
     bf16 = jnp.bfloat16
     anyspace = pl.BlockSpec(memory_space=pl.ANY)
-    return tuple(pl.pallas_call(
+    gin, gw = pl.pallas_call(
         functools.partial(kernel, ni, nj),
         out_shape=(
             pltpu.VMEM((tok, width), bf16),
@@ -241,6 +288,8 @@
             pltpu.VMEM((half, kv), jnp.int32),
             pltpu.VMEM((1, half // 2), jnp.float32),
             pltpu.VMEM((half, kv), bf16),
+            pltpu.VMEM((half, kv), bf16),
+            pltpu.VMEM((1, half // 2), jnp.float32),
             pltpu.VMEM((nz, group * tok, blk), bf16),
             pltpu.VMEM((ni, 2 * tok, half), bf16),
             pltpu.VMEM((max(nz - 1, 1), blk, kv), bf16),
@@ -250,9 +299,21 @@
             dma((group, nz)), dma((group, nz)),
             dma((group,)), dma((group,)),
             dma((nz,)), dma((nz,)),
+            dma((nz,)), dma((nz,)), dma, dma,
+            pltpu.SemaphoreType.REGULAR, pltpu.SemaphoreType.REGULAR,
         ],
         compiler_params=pltpu.CompilerParams(collective_id=0, has_side_effects=True),
-    )(acts, grad_out, codes, scales.reshape(1, -1)))
+    )(acts, grad_out, codes, scales.reshape(1, -1))
+    return tuple(pl.pallas_call(
+        leave,
+        out_shape=(
+            jax.ShapeDtypeStruct((tok, width), bf16),
+            jax.ShapeDtypeStruct((blk, kv), jnp.float32),
+        ),
+        in_specs=[anyspace] * 2,
+        out_specs=(anyspace,) * 2,
+        scratch_shapes=[dma((2,))],
+    )(*(pltpu.with_memory_space_constraint(x, pltpu.VMEM) for x in (gin, gw))))
 
 
 def plain(acts, grad_out, codes, scales):

time: 37.6 us -> 40.6 us (1.080)
  the two profiles are of different devices: /device:TPU:0 before, /device:TPU:12 now
where the time goes in v1:
time: 40.6 us; the launch traced here: 40.5 us
  Pallas kernels  39.8 us (98%)
  between operations  0.64 us (2%)
    pallas_call x1, Pallas kernels, fused(): pl.pallas_call(functools.partial(kernel, ni, nj), out_shape=(pltpu.VMEM((...  38.8 us
    pallas_call x1, Pallas kernels, fused(): pl.pallas_call(leave, out_shape=(jax.ShapeDtypeStruct((tok, width), bf16)...  1.07 us

profile of v1, /device:TPU:12, one launch (start us, length us, event | category | flops | bytes accessed | tf_op | source)
XLA Modules:
  0.0 40.5 jit_solution(17346086624726776959)
XLA Ops:
  0.6 38.8 %shard_map.59 = (bf16[128,4096]{1,0:T(8,128)(2,1)S(1)}, f32[128,512]{1,0:T(8,128)S(1)}) custom-call(bf16[128,4096]{1,0:T(8,128)(2,1)} %acts.1, bf16[128,512]{1,0:T(8,128)(2,1)} %go.1, s32[1024,512]{1,0:T(8,128)} %codes.1, f32[1,512]{1,0:T(1,128)} %bitcast.1), custom_call_target="tpu_custom_call" | custom-call | tf_op jit(solution)/shard_map/pallas_call | solution.py:277
  39.4 1.1 %shard_map.60 = (bf16[128,4096]{1,0:T(8,128)(2,1)}, f32[128,512]{1,0:T(8,128)}) custom-call(bf16[128,4096]{1,0:T(8,128)(2,1)S(1)} %get-tuple-element.4.gin, f32[128,512]{1,0:T(8,128)S(1)} %get-tuple-element.5.gw), custom_call_target="tpu_custom_call" | custom-call | tf_op jit(solution)/shard_map/pallas_call | solution.py:307

commit v2 on v1

--- a/solution.py
+++ b/solution.py
@@ -37,9 +37,9 @@
 
 def kernel(
     ni, nj, acts, go, codes, scales, gin, gw,
-    go_all, acts_v, codes_v, scale_v, code_b, code_d, scale_d, ac, pieces, part, rs,
+    go_all, acts_v, codes_v, scale_v, code_b, code_d, scale_d, ac, pieces, part, rs, held, ms,
     load_sem, go_send, go_recv, gh_send, gh_recv, fw_send, a_send, a_recv, p_send, p_recv,
-    r_send, r_recv, w_send, w_recv, s_send, s_recv, plane_sem, line_sem,
+    r_send, r_recv, m_recv, w_send, w_recv, s_send, s_recv, plane_sem, line_sem,
 ):
     tok, width = acts.shape
     rows = codes.shape[0]
@@ -56,6 +56,12 @@
     near, diag = (1, 2), 3
     dd = peers[diag]
     cores = (c, oc)
+    pair = z // 2
+    inner = lax.rem(z, 2) != pair
+    mate = 2 * pair + 1 - lax.rem(z, 2)
+    far_outer = 3 * (1 - pair)
+    far_inner = 2 - pair
+    order = [far_outer, far_inner, mate, z]
 
     def dev(ii, zz, cc):
         return {"intra": ii, "inter": 2 * zz + cc}
@@ -134,7 +140,6 @@
     send(code_b.at[quarter(z)], code_d.at[quarter(z)], w_send.at[0], w_recv.at[z], dev(dd, z, c))
 
     load_acts.wait()
-    order = [lax.rem(z + k, nz) for k in range(1, nz)] + [z]
     own = []
 
     def send_columns(h):
@@ -151,8 +156,6 @@
                     cp.start()
                     own.append(cp)
 
-    send_columns(order[0])
-
     def wait_go(m):
         arrived(go_slot(m), go_send.at[0], go_recv.at[m])
 
@@ -161,7 +164,7 @@
         wait_go(m)
         send(go_half(m, n), go_half(m, n), gh_send.at[n], gh_recv.at[n], dev(peers[diag ^ d], z, c))
         send(go_slot(m), go_slot(m), fw_send.at[d], go_recv.at[m], dev(i, z, oc))
-    for h in order[1:]:
+    for h in order:
         send_columns(h)
 
     def pieces_of(ii, code, scale):
@@ -196,10 +199,21 @@
     def _():
         pl.semaphore_wait(line_sem, 1)
 
-    arrived(code_d.at[quarter(z)], w_send.at[0], w_recv.at[z])
-    for k in range(1, nz):
-        send(code_d.at[quarter(z)], code_d.at[quarter(z)], w_send.at[k], w_recv.at[z],
-             dev(i, lax.rem(z + k, nz), c))
+    def hop(n, h, to):
+        return rdma(code_d.at[quarter(h)], code_d.at[quarter(h)], w_send.at[n], w_recv.at[h], dev(i, to, c))
+
+    def landed(h):
+        arrived(code_d.at[quarter(h)], w_send.at[0], w_recv.at[h])
+
+    to_mate = hop(1, z, mate)
+    relays = [hop(2, z, far_inner), hop(3, mate, far_inner), hop(4, far_inner, mate), hop(5, far_outer, mate)]
+    landed(z)
+    to_mate.start()
+    sends.append(to_mate)
+
+    @pl.when(inner)
+    def _():
+        relays[0].start()
 
     m = 2 * dd + c
     for n in range(2):
@@ -209,36 +223,78 @@
     far_scale = lane_scale(scale_d[...], half)
     wait_go(2 * dd + oc)
 
-    mine = None
-    for n, h in enumerate(order):
+    @pl.when(inner)
+    def _():
+        landed(mate)
+        relays[1].start()
+        landed(far_inner)
+        relays[2].start()
+
+    def term_of(n):
+        h = order[n]
         own[n].wait()
         for d in range(ni):
             for k, cc in enumerate(cores):
                 if d or k:
                     m = 2 * peers[d] + cc
                     arrived(ac_slot(h, m), a_send.at[m, h], a_recv.at[m, h])
-        term = lax.dot_general(
+        return lax.dot_general(
             ac[h], go_all[...], (((0,), (0,)), ((), ())), preferred_element_type=jnp.float32
         )
-        if n < nz - 1:
+
+    def pass_on(n, dst, recv, to):
+        return rdma(part.at[n], dst, r_send.at[n], recv, dev(i, to, c))
+
+    to_inner = [pass_on(n, ms.at[n], m_recv.at[n], mate) for n in range(2)]
+    across = [pass_on(n, rs.at[1], r_recv.at[1], order[n]) for n in range(2)]
+
+    def first_terms(n):
+        term = term_of(n)
+
+        @pl.when(inner)
+        def _():
+            held[n] = term
+
+        @pl.when(jnp.logical_not(inner))
+        def _():
             part[n] = term.astype(jnp.bfloat16)
-            send(part.at[n], rs.at[z], r_send.at[n], r_recv.at[z], dev(i, h, c))
-        else:
-            mine = term
-
-    for k in range(1, nz):
-        h = lax.rem(z + k, nz)
-        arrived(code_d.at[quarter(h)], w_send.at[k], w_recv.at[h])
+            to_inner[n].start()
+
+    def merge(n):
+        @pl.when(inner)
+        def _():
+            arrived(ms.at[n], r_send.at[n], m_recv.at[n])
+            part[n] = (held[n] + ms[n].astype(jnp.float32)).astype(jnp.bfloat16)
+            across[n].start()
+
+    first_terms(0)
+    first_terms(1)
+
+    @pl.when(inner)
+    def _():
+        landed(far_outer)
+        relays[3].start()
+
+    merge(0)
+    part[2] = term_of(2).astype(jnp.bfloat16)
+    send(part.at[2], rs.at[0], r_send.at[2], r_recv.at[0], dev(i, mate, c))
+    merge(1)
+    mine = term_of(3)
+
+    @pl.when(jnp.logical_not(inner))
+    def _():
+        for h in order[:3]:
+            landed(h)
+
     pieces[diag] = pieces_of(i, code_d, far_scale)
     far = gin.at[:, cols_of(dd, c)]
     send(piece(diag, oc), far, p_send.at[2 * dd + c], p_recv.at[2 * dd + c], dev(i, z, oc))
     keep_far = pltpu.make_async_copy(piece(diag, c), far, load_sem.at[0])
     keep_far.start()
 
-    for k in range(1, nz):
-        h = lax.rem(z + k, nz)
-        arrived(rs.at[h], r_send.at[0], r_recv.at[h])
-        mine = mine + rs[h].astype(jnp.float32)
+    for n in range(2):
+        arrived(rs.at[n], r_send.at[n], r_recv.at[n])
+        mine = mine + rs[n].astype(jnp.float32)
     gw[...] = mine * (1.0 / math.sqrt(tok * ni * nj))
 
     keep.wait()
@@ -250,8 +306,13 @@
                 block = gin.at[:, cols_of(ii, cc)]
                 arrived(block, p_send.at[2 * ii + cc], p_recv.at[2 * ii + cc])
     arrived(gin.at[:, cols_of(dd, oc)], p_send.at[2 * dd + oc], p_recv.at[2 * dd + oc])
-    for cp in sends:
+    for cp in sends + across:
         cp.wait_send()
+
+    @pl.when(inner)
+    def _():
+        for cp in relays:
+            cp.wait_send()
 
 
 def leave(gin, gw, gin_out, gw_out, sem):
@@ -292,14 +353,16 @@
             pltpu.VMEM((1, half // 2), jnp.float32),
             pltpu.VMEM((nz, group * tok, blk), bf16),
             pltpu.VMEM((ni, 2 * tok, half), bf16),
-            pltpu.VMEM((max(nz - 1, 1), blk, kv), bf16),
-            pltpu.VMEM((nz, blk, kv), bf16),
+            pltpu.VMEM((3, blk, kv), bf16),
+            pltpu.VMEM((2, blk, kv), bf16),
+            pltpu.VMEM((2, blk, kv), jnp.float32),
+            pltpu.VMEM((2, blk, kv), bf16),
             dma((4,)),
             dma((ni,)), dma((group,)), dma((2,)), dma((2,)), dma((ni,)),
             dma((group, nz)), dma((group, nz)),
             dma((group,)), dma((group,)),
-            dma((nz,)), dma((nz,)),
-            dma((nz,)), dma((nz,)), dma, dma,
+            dma((3,)), dma((2,)), dma((2,)),
+            dma((6,)), dma((nz,)), dma, dma,
             pltpu.SemaphoreType.REGULAR, pltpu.SemaphoreType.REGULAR,
         ],
         compiler_params=pltpu.CompilerParams(collective_id=0, has_side_effects=True),
@@ -347,7 +410,7 @@
     def per_device(acts, grad_out, codes, scales):
         rows = codes.shape[0]
         aligned = rows % (nj * 128) == 0 and rows % 512 == 0 and acts.shape[0] % 16 == 0
-        if aligned and nj % 2 == 0 and ni == 4 and acts.shape[1] == ni * rows:
+        if aligned and nj == 8 and ni == 4 and acts.shape[1] == ni * rows:
             return fused(ni, nj, acts, grad_out, codes, scales)
         return plain(acts, grad_out, codes, scales)
 

time: 40.6 us -> 35.1 us (0.86)
  the two profiles are of different devices: /device:TPU:12 before, /device:TPU:0 now
where the time goes in v2:
time: 35.1 us; the launch traced here: 34.9 us
  Pallas kernels  34.3 us (98%)
  between operations  0.64 us (2%)
    pallas_call x1, Pallas kernels, fused(): pl.pallas_call(functools.partial(kernel, ni, nj), out_shape=(pltpu.VMEM((...  33.2 us
    pallas_call x1, Pallas kernels, fused(): pl.pallas_call(leave, out_shape=(jax.ShapeDtypeStruct((tok, width), bf16)...  1.07 us

profile of v2, /device:TPU:0, one launch (start us, length us, event | category | flops | bytes accessed | tf_op | source)
XLA Modules:
  0.0 34.9 jit_solution(5100164589056501899)
XLA Ops:
  0.6 33.2 %shard_map.59 = (bf16[128,4096]{1,0:T(8,128)(2,1)S(1)}, f32[128,512]{1,0:T(8,128)S(1)}) custom-call(bf16[128,4096]{1,0:T(8,128)(2,1)} %acts.1, bf16[128,512]{1,0:T(8,128)(2,1)} %go.1, s32[1024,512]{1,0:T(8,128)} %codes.1, f32[1,512]{1,0:T(1,128)} %bitcast.1), custom_call_target="tpu_custom_call" | custom-call | tf_op jit(solution)/shard_map/pallas_call | solution.py:338
  33.9 1.1 %shard_map.60 = (bf16[128,4096]{1,0:T(8,128)(2,1)}, f32[128,512]{1,0:T(8,128)}) custom-call(bf16[128,4096]{1,0:T(8,128)(2,1)S(1)} %get-tuple-element.4.gin, f32[128,512]{1,0:T(8,128)S(1)} %get-tuple-element.5.gw), custom_call_target="tpu_custom_call" | custom-call | tf_op jit(solution)/shard_map/pallas_call | solution.py:370

commit v3 on v2

--- a/solution.py
+++ b/solution.py
@@ -38,7 +38,7 @@
 def kernel(
     ni, nj, acts, go, codes, scales, gin, gw,
     go_all, acts_v, codes_v, scale_v, code_b, code_d, scale_d, ac, pieces, part, rs, held, ms,
-    load_sem, go_send, go_recv, gh_send, gh_recv, fw_send, a_send, a_recv, p_send, p_recv,
+    load_sem, go_send, go_recv, pair_recv, gh_send, gh_recv, fw_send, a_send, a_recv, p_send, p_recv,
     r_send, r_recv, m_recv, w_send, w_recv, s_send, s_recv, plane_sem, line_sem,
 ):
     tok, width = acts.shape
@@ -128,9 +128,12 @@
     def _():
         pl.semaphore_wait(plane_sem, 1)
 
-    for d in near:
-        send(go_slot(me), go_slot(me), go_send.at[d], go_recv.at[me], dev(peers[d], z, c))
-    send(go_slot(me), go_slot(me), go_send.at[0], go_recv.at[me], dev(i, z, oc))
+    def send_go(late):
+        for n, d in enumerate(near):
+            part_go = go_half(me, 1 - n if late else n)
+            send(part_go, part_go, go_send.at[d, late], go_recv.at[me, late], dev(peers[d], z, c))
+
+    send_go(0)
 
     load_codes.wait()
     code_b[...] = codes_v[...].astype(jnp.float32).astype(jnp.bfloat16)
@@ -138,6 +141,8 @@
     send(scale_v, scale_d, s_send, s_recv, dev(dd, z, c))
     row_scale = lane_scale(scale_v[...], half)
     send(code_b.at[quarter(z)], code_d.at[quarter(z)], w_send.at[0], w_recv.at[z], dev(dd, z, c))
+    send_go(1)
+    send(go_slot(me), go_slot(me), fw_send.at[0], pair_recv.at[i], dev(i, z, oc))
 
     load_acts.wait()
     own = []
@@ -156,16 +161,50 @@
                     cp.start()
                     own.append(cp)
 
-    def wait_go(m):
-        arrived(go_slot(m), go_send.at[0], go_recv.at[m])
+    def wait_pair(ii):
+        arrived(go_slot(2 * ii + oc), fw_send.at[0], pair_recv.at[ii])
 
     for n, d in enumerate(near):
         m = 2 * peers[d] + c
-        wait_go(m)
+        arrived(go_half(m, n), go_send.at[d, 0], go_recv.at[m, 0])
         send(go_half(m, n), go_half(m, n), gh_send.at[n], gh_recv.at[n], dev(peers[diag ^ d], z, c))
-        send(go_slot(m), go_slot(m), fw_send.at[d], go_recv.at[m], dev(i, z, oc))
     for h in order:
         send_columns(h)
+
+    @pl.when(c == 1)
+    def _():
+        pl.semaphore_wait(barrier, 2 * (nz - 1))
+        pl.semaphore_signal(line_sem, inc=1, device_id=dev(i, z, 0), device_id_type=MESH)
+
+    @pl.when(c == 0)
+    def _():
+        pl.semaphore_wait(line_sem, 1)
+
+    def hop(n, h, to):
+        return rdma(code_d.at[quarter(h)], code_d.at[quarter(h)], w_send.at[n], w_recv.at[h], dev(i, to, c))
+
+    def landed(h):
+        arrived(code_d.at[quarter(h)], w_send.at[0], w_recv.at[h])
+
+    to_mate = hop(1, z, mate)
+    relays = [hop(2, z, far_inner), hop(3, mate, far_inner), hop(4, far_inner, mate), hop(5, far_outer, mate)]
+    landed(z)
+    to_mate.start()
+    sends.append(to_mate)
+
+    @pl.when(inner)
+    def _():
+        relays[0].start()
+
+    for n, d in enumerate(near):
+        m = 2 * peers[d] + c
+        arrived(go_half(m, 1 - n), go_send.at[d, 1], go_recv.at[m, 1])
+        send(go_slot(m), go_slot(m), fw_send.at[d], pair_recv.at[peers[d]], dev(i, z, oc))
+
+    m = 2 * dd + c
+    for n in range(2):
+        arrived(go_half(m, n), gh_send.at[n], gh_recv.at[n])
+    send(go_slot(m), go_slot(m), fw_send.at[diag], pair_recv.at[dd], dev(i, z, oc))
 
     def pieces_of(ii, code, scale):
         pair = go_all[pl.ds(pl.multiple_of(2 * ii * tok, 2 * tok), 2 * tok)]
@@ -179,49 +218,20 @@
 
     for d in near:
         ii = peers[d]
-        wait_go(2 * ii + oc)
+        wait_pair(ii)
         pieces[d] = pieces_of(ii, code_b, row_scale)
         for cc in cores:
             m = 2 * ii + cc
             send(piece(d, cc), gin.at[:, cols_of(i, c)], p_send.at[m], p_recv.at[me], dev(ii, z, cc))
-    wait_go(2 * i + oc)
+    wait_pair(i)
     pieces[0] = pieces_of(i, code_b, row_scale)
     send(piece(0, oc), gin.at[:, cols_of(i, c)], p_send.at[2 * i + oc], p_recv.at[me], dev(i, z, oc))
     keep = pltpu.make_async_copy(piece(0, c), gin.at[:, cols_of(i, c)], p_recv.at[me])
     keep.start()
 
-    @pl.when(c == 1)
-    def _():
-        pl.semaphore_wait(barrier, 2 * (nz - 1))
-        pl.semaphore_signal(line_sem, inc=1, device_id=dev(i, z, 0), device_id_type=MESH)
-
-    @pl.when(c == 0)
-    def _():
-        pl.semaphore_wait(line_sem, 1)
-
-    def hop(n, h, to):
-        return rdma(code_d.at[quarter(h)], code_d.at[quarter(h)], w_send.at[n], w_recv.at[h], dev(i, to, c))
-
-    def landed(h):
-        arrived(code_d.at[quarter(h)], w_send.at[0], w_recv.at[h])
-
-    to_mate = hop(1, z, mate)
-    relays = [hop(2, z, far_inner), hop(3, mate, far_inner), hop(4, far_inner, mate), hop(5, far_outer, mate)]
-    landed(z)
-    to_mate.start()
-    sends.append(to_mate)
-
-    @pl.when(inner)
-    def _():
-        relays[0].start()
-
-    m = 2 * dd + c
-    for n in range(2):
-        arrived(go_half(m, n), gh_send.at[n], gh_recv.at[n])
-    send(go_slot(m), go_slot(m), fw_send.at[diag], go_recv.at[m], dev(i, z, oc))
     arrived(scale_d, s_send, s_recv)
     far_scale = lane_scale(scale_d[...], half)
-    wait_go(2 * dd + oc)
+    wait_pair(dd)
 
     @pl.when(inner)
     def _():
@@ -358,7 +368,7 @@
             pltpu.VMEM((2, blk, kv), jnp.float32),
             pltpu.VMEM((2, blk, kv), bf16),
             dma((4,)),
-            dma((ni,)), dma((group,)), dma((2,)), dma((2,)), dma((ni,)),
+            dma((ni, 2)), dma((group, 2)), dma((ni,)), dma((2,)), dma((2,)), dma((ni,)),
             dma((group, nz)), dma((group, nz)),
             dma((group,)), dma((group,)),
             dma((3,)), dma((2,)), dma((2,)),

time: 35.1 us -> 33.9 us (0.966)
  Pallas kernels: 34.3 us -> 33.1 us
    pallas_call x1, Pallas kernels: 33.2 us -> 32.1 us  [fused(): pl.pallas_call(functools.partial(kernel, ni, nj), out_shape=(pltpu.VMEM((...]
where the time goes in v3:
time: 33.9 us; the launch traced here: 33.8 us
  Pallas kernels  33.1 us (98%)
  between operations  0.64 us (2%)
    pallas_call x1, Pallas kernels, fused(): pl.pallas_call(functools.partial(kernel, ni, nj), out_shape=(pltpu.VMEM((...  32.1 us
    pallas_call x1, Pallas kernels, fused(): pl.pallas_call(leave, out_shape=(jax.ShapeDtypeStruct((tok, width), bf16)...  1.07 us

profile of v3, /device:TPU:0, one launch (start us, length us, event | category | flops | bytes accessed | tf_op | source)
XLA Modules:
  0.0 33.8 jit_solution(7018994914990046551)
XLA Ops:
  0.6 32.1 %shard_map.59 = (bf16[128,4096]{1,0:T(8,128)(2,1)S(1)}, f32[128,512]{1,0:T(8,128)S(1)}) custom-call(bf16[128,4096]{1,0:T(8,128)(2,1)} %acts.1, bf16[128,512]{1,0:T(8,128)(2,1)} %go.1, s32[1024,512]{1,0:T(8,128)} %codes.1, f32[1,512]{1,0:T(1,128)} %bitcast.1), custom_call_target="tpu_custom_call" | custom-call | tf_op jit(solution)/shard_map/pallas_call | solution.py:348
  32.7 1.1 %shard_map.60 = (bf16[128,4096]{1,0:T(8,128)(2,1)}, f32[128,512]{1,0:T(8,128)}) custom-call(bf16[128,4096]{1,0:T(8,128)(2,1)S(1)} %get-tuple-element.4.gin, f32[128,512]{1,0:T(8,128)S(1)} %get-tuple-element.5.gw), custom_call_target="tpu_custom_call" | custom-call | tf_op jit(solution)/shard_map/pallas_call | solution.py:380

commit v4 on v3

--- a/solution.py
+++ b/solution.py
@@ -38,8 +38,8 @@
 def kernel(
     ni, nj, acts, go, codes, scales, gin, gw,
     go_all, acts_v, codes_v, scale_v, code_b, code_d, scale_d, ac, pieces, part, rs, held, ms,
-    load_sem, go_send, go_recv, pair_recv, gh_send, gh_recv, fw_send, a_send, a_recv, p_send, p_recv,
-    r_send, r_recv, m_recv, w_send, w_recv, s_send, s_recv, plane_sem, line_sem,
+    load_sem, go_send, go_recv, pair_recv, gh_recv, a_send, a_recv, p_send, p_recv,
+    r_send, r_recv, m_recv, w_send, w_recv, s_send, s_recv, near_sem, diag_sem, line_sem,
 ):
     tok, width = acts.shape
     rows = codes.shape[0]
@@ -71,15 +71,14 @@
             src_ref=src, dst_ref=dst, send_sem=s, recv_sem=r, device_id=where, device_id_type=MESH
         )
 
-    def arrived(ref, s, r):
-        rdma(ref, ref, s, r, dev(i, z, oc)).wait_recv()
-
-    sends = []
+    def arrived(ref, r):
+        rdma(ref, ref, r, r, dev(i, z, oc)).wait_recv()
+
+    def drained(ref, s):
+        rdma(ref, ref, s, s, dev(i, z, oc)).wait_send()
 
     def send(*args):
-        cp = rdma(*args)
-        cp.start()
-        sends.append(cp)
+        rdma(*args).start()
 
     def go_slot(m):
         return go_all.at[pl.ds(pl.multiple_of(m * tok, tok), tok)]
@@ -99,7 +98,7 @@
     half_start = pl.multiple_of(c * half, half)
     sc_start = pl.multiple_of(c * (half // 2), half // 2)
     barrier = pltpu.get_barrier_semaphore()
-    for d in range(1, ni):
+    for d in near:
         pl.semaphore_signal(barrier, inc=1, device_id=dev(peers[d], z, 0), device_id_type=MESH)
 
     @pl.when(c == 1)
@@ -121,55 +120,53 @@
 
     @pl.when(c == 0)
     def _():
-        pl.semaphore_wait(barrier, 2 * ni - 1)
-        pl.semaphore_signal(plane_sem, inc=1, device_id=dev(i, z, 1), device_id_type=MESH)
+        pl.semaphore_wait(barrier, 2 * len(near) + 1)
+        pl.semaphore_signal(near_sem, inc=1, device_id=dev(i, z, 1), device_id_type=MESH)
 
     @pl.when(c == 1)
     def _():
-        pl.semaphore_wait(plane_sem, 1)
+        pl.semaphore_wait(near_sem, 1)
 
     def send_go(late):
         for n, d in enumerate(near):
             part_go = go_half(me, 1 - n if late else n)
-            send(part_go, part_go, go_send.at[d, late], go_recv.at[me, late], dev(peers[d], z, c))
+            send(part_go, part_go, go_send, go_recv.at[n, late], dev(peers[d], z, c))
 
     send_go(0)
+    pl.semaphore_signal(diag_sem, inc=1, device_id=dev(peers[near[0]], z, c), device_id_type=MESH)
 
     load_codes.wait()
     code_b[...] = codes_v[...].astype(jnp.float32).astype(jnp.bfloat16)
     load_scale.wait()
+    pl.semaphore_wait(diag_sem, 1)
     send(scale_v, scale_d, s_send, s_recv, dev(dd, z, c))
     row_scale = lane_scale(scale_v[...], half)
     send(code_b.at[quarter(z)], code_d.at[quarter(z)], w_send.at[0], w_recv.at[z], dev(dd, z, c))
     send_go(1)
-    send(go_slot(me), go_slot(me), fw_send.at[0], pair_recv.at[i], dev(i, z, oc))
+    send(go_slot(me), go_slot(me), go_send, pair_recv.at[0], dev(i, z, oc))
 
     load_acts.wait()
-    own = []
-
-    def send_columns(h):
+
+    def send_columns(n):
+        h = order[n]
         for d in near + (0, diag):
             for k, cc in enumerate(cores):
                 ii = peers[d]
                 col = pl.multiple_of(ii * rows + (2 * h + cc) * blk, blk)
-                src = acts_v.at[:, pl.ds(col, blk)]
                 if d or k:
-                    m = 2 * ii + cc
-                    send(src, ac_slot(h, me), a_send.at[m, h], a_recv.at[me, h], dev(ii, z, cc))
+                    send(acts_v.at[:, pl.ds(col, blk)], ac_slot(h, me), a_send, a_recv.at[n], dev(ii, z, cc))
                 else:
-                    cp = pltpu.make_async_copy(src, ac_slot(h, me), a_recv.at[me, h])
-                    cp.start()
-                    own.append(cp)
-
-    def wait_pair(ii):
-        arrived(go_slot(2 * ii + oc), fw_send.at[0], pair_recv.at[ii])
+                    ac_slot(h, me)[...] = acts_v[:, pl.ds(col, blk)]
+
+    def wait_pair(d):
+        arrived(go_slot(2 * peers[d] + oc), pair_recv.at[d])
 
     for n, d in enumerate(near):
         m = 2 * peers[d] + c
-        arrived(go_half(m, n), go_send.at[d, 0], go_recv.at[m, 0])
-        send(go_half(m, n), go_half(m, n), gh_send.at[n], gh_recv.at[n], dev(peers[diag ^ d], z, c))
-    for h in order:
-        send_columns(h)
+        arrived(go_half(m, n), go_recv.at[n, 0])
+        send(go_half(m, n), go_half(m, n), go_send, gh_recv, dev(peers[diag ^ d], z, c))
+    for n in range(nz):
+        send_columns(n)
 
     @pl.when(c == 1)
     def _():
@@ -181,30 +178,26 @@
         pl.semaphore_wait(line_sem, 1)
 
     def hop(n, h, to):
-        return rdma(code_d.at[quarter(h)], code_d.at[quarter(h)], w_send.at[n], w_recv.at[h], dev(i, to, c))
+        send(code_d.at[quarter(h)], code_d.at[quarter(h)], w_send.at[n], w_recv.at[h], dev(i, to, c))
 
     def landed(h):
-        arrived(code_d.at[quarter(h)], w_send.at[0], w_recv.at[h])
-
-    to_mate = hop(1, z, mate)
-    relays = [hop(2, z, far_inner), hop(3, mate, far_inner), hop(4, far_inner, mate), hop(5, far_outer, mate)]
+        arrived(code_d.at[quarter(h)], w_recv.at[h])
+
     landed(z)
-    to_mate.start()
-    sends.append(to_mate)
+    hop(0, z, mate)
 
     @pl.when(inner)
     def _():
-        relays[0].start()
+        hop(1, z, far_inner)
 
     for n, d in enumerate(near):
         m = 2 * peers[d] + c
-        arrived(go_half(m, 1 - n), go_send.at[d, 1], go_recv.at[m, 1])
-        send(go_slot(m), go_slot(m), fw_send.at[d], pair_recv.at[peers[d]], dev(i, z, oc))
+        arrived(go_half(m, 1 - n), go_recv.at[n, 1])
+        send(go_slot(m), go_slot(m), go_send, pair_recv.at[d], dev(i, z, oc))
 
     m = 2 * dd + c
-    for n in range(2):
-        arrived(go_half(m, n), gh_send.at[n], gh_recv.at[n])
-    send(go_slot(m), go_slot(m), fw_send.at[diag], pair_recv.at[dd], dev(i, z, oc))
+    arrived(go_slot(m), gh_recv)
+    send(go_slot(m), go_slot(m), go_send, pair_recv.at[diag], dev(i, z, oc))
 
     def pieces_of(ii, code, scale):
         pair = go_all[pl.ds(pl.multiple_of(2 * ii * tok, 2 * tok), 2 * tok)]
@@ -216,47 +209,41 @@
     def piece(n, cc):
         return pieces.at[n, pl.ds(pl.multiple_of(cc * tok, tok), tok)]
 
+    def own_piece(n, ii):
+        gin[:, cols_of(ii, c)] = piece(n, c)[...]
+        send(piece(n, oc), gin.at[:, cols_of(ii, c)], p_send, p_recv, dev(i, z, oc))
+
     for d in near:
         ii = peers[d]
-        wait_pair(ii)
+        wait_pair(d)
         pieces[d] = pieces_of(ii, code_b, row_scale)
         for cc in cores:
-            m = 2 * ii + cc
-            send(piece(d, cc), gin.at[:, cols_of(i, c)], p_send.at[m], p_recv.at[me], dev(ii, z, cc))
-    wait_pair(i)
+            send(piece(d, cc), gin.at[:, cols_of(i, c)], p_send, p_recv, dev(ii, z, cc))
+    wait_pair(0)
     pieces[0] = pieces_of(i, code_b, row_scale)
-    send(piece(0, oc), gin.at[:, cols_of(i, c)], p_send.at[2 * i + oc], p_recv.at[me], dev(i, z, oc))
-    keep = pltpu.make_async_copy(piece(0, c), gin.at[:, cols_of(i, c)], p_recv.at[me])
-    keep.start()
-
-    arrived(scale_d, s_send, s_recv)
+    own_piece(0, i)
+
+    arrived(scale_d, s_recv)
     far_scale = lane_scale(scale_d[...], half)
-    wait_pair(dd)
+    wait_pair(diag)
 
     @pl.when(inner)
     def _():
         landed(mate)
-        relays[1].start()
+        hop(1, mate, far_inner)
+        hop(1, mate, far_outer)
         landed(far_inner)
-        relays[2].start()
+        hop(1, far_inner, mate)
 
     def term_of(n):
         h = order[n]
-        own[n].wait()
-        for d in range(ni):
-            for k, cc in enumerate(cores):
-                if d or k:
-                    m = 2 * peers[d] + cc
-                    arrived(ac_slot(h, m), a_send.at[m, h], a_recv.at[m, h])
+        arrived(ac.at[h, pl.ds(0, (2 * ni - 1) * tok)], a_recv.at[n])
         return lax.dot_general(
             ac[h], go_all[...], (((0,), (0,)), ((), ())), preferred_element_type=jnp.float32
         )
 
     def pass_on(n, dst, recv, to):
-        return rdma(part.at[n], dst, r_send.at[n], recv, dev(i, to, c))
-
-    to_inner = [pass_on(n, ms.at[n], m_recv.at[n], mate) for n in range(2)]
-    across = [pass_on(n, rs.at[1], r_recv.at[1], order[n]) for n in range(2)]
+        send(part.at[n], dst, r_send, recv, dev(i, to, c))
 
     def first_terms(n):
         term = term_of(n)
@@ -268,61 +255,52 @@
         @pl.when(jnp.logical_not(inner))
         def _():
             part[n] = term.astype(jnp.bfloat16)
-            to_inner[n].start()
+            pass_on(n, ms.at[n], m_recv.at[n], mate)
 
     def merge(n):
         @pl.when(inner)
         def _():
-            arrived(ms.at[n], r_send.at[n], m_recv.at[n])
+            arrived(ms.at[n], m_recv.at[n])
             part[n] = (held[n] + ms[n].astype(jnp.float32)).astype(jnp.bfloat16)
-            across[n].start()
+            pass_on(n, rs.at[1], r_recv, order[n])
 
     first_terms(0)
     first_terms(1)
 
-    @pl.when(inner)
-    def _():
-        landed(far_outer)
-        relays[3].start()
-
     merge(0)
     part[2] = term_of(2).astype(jnp.bfloat16)
-    send(part.at[2], rs.at[0], r_send.at[2], r_recv.at[0], dev(i, mate, c))
+    pass_on(2, rs.at[0], r_recv, mate)
     merge(1)
     mine = term_of(3)
 
     @pl.when(jnp.logical_not(inner))
     def _():
-        for h in order[:3]:
-            landed(h)
+        landed(mate)
+        landed(far_inner)
+
+    landed(far_outer)
 
     pieces[diag] = pieces_of(i, code_d, far_scale)
-    far = gin.at[:, cols_of(dd, c)]
-    send(piece(diag, oc), far, p_send.at[2 * dd + c], p_recv.at[2 * dd + c], dev(i, z, oc))
-    keep_far = pltpu.make_async_copy(piece(diag, c), far, load_sem.at[0])
-    keep_far.start()
-
+    own_piece(diag, dd)
+
+    arrived(rs, r_recv)
     for n in range(2):
-        arrived(rs.at[n], r_send.at[n], r_recv.at[n])
         mine = mine + rs[n].astype(jnp.float32)
     gw[...] = mine * (1.0 / math.sqrt(tok * ni * nj))
 
-    keep.wait()
-    keep_far.wait()
-    for d in (0,) + near:
-        for k, cc in enumerate(cores):
-            if d or k:
-                ii = peers[d]
-                block = gin.at[:, cols_of(ii, cc)]
-                arrived(block, p_send.at[2 * ii + cc], p_recv.at[2 * ii + cc])
-    arrived(gin.at[:, cols_of(dd, oc)], p_send.at[2 * dd + oc], p_recv.at[2 * dd + oc])
-    for cp in sends + across:
-        cp.wait_send()
+    drained(go_all.at[pl.ds(0, (2 * ni - 1) * tok)], go_send)
+    drained(acts_v.at[:, pl.ds(0, nz * (2 * ni - 1) * blk)], a_send)
+    drained(part, r_send)
+    drained(code_d.at[pl.ds(0, 2 * blk)], w_send.at[0])
+    drained(scale_v, s_send)
 
     @pl.when(inner)
     def _():
-        for cp in relays:
-            cp.wait_send()
+        drained(code_d, w_send.at[1])
+
+    pieces_all = gin.at[:, pl.ds(0, 6 * half)]
+    drained(pieces_all, p_send)
+    arrived(pieces_all, p_recv)
 
 
 def leave(gin, gw, gin_out, gw_out, sem):
@@ -368,12 +346,11 @@
             pltpu.VMEM((2, blk, kv), jnp.float32),
             pltpu.VMEM((2, blk, kv), bf16),
             dma((4,)),
-            dma((ni, 2)), dma((group, 2)), dma((ni,)), dma((2,)), dma((2,)), dma((ni,)),
-            dma((group, nz)), dma((group, nz)),
-            dma((group,)), dma((group,)),
-            dma((3,)), dma((2,)), dma((2,)),
-            dma((6,)), dma((nz,)), dma, dma,
-            pltpu.SemaphoreType.REGULAR, pltpu.SemaphoreType.REGULAR,
+            dma, dma((2, 2)), dma((ni,)), dma,
+            dma, dma((nz,)), dma, dma,
+            dma, dma, dma((2,)),
+            dma((2,)), dma((nz,)), dma, dma,
+            *[pltpu.SemaphoreType.REGULAR] * 3,
         ],
         compiler_params=pltpu.CompilerParams(collective_id=0, has_side_effects=True),
     )(acts, grad_out, codes, scales.reshape(1, -1))

time: 33.9 us -> 34 us (level)
  no operation moved by 1% of the time
where the time goes in v4:
time: 34 us; the launch traced here: 33.9 us
  Pallas kernels  33.2 us (98%)
  between operations  0.64 us (2%)
    pallas_call x1, Pallas kernels, fused(): pl.pallas_call(functools.partial(kernel, ni, nj), out_shape=(pltpu.VMEM((...  32.2 us
    pallas_call x1, Pallas kernels, fused(): pl.pallas_call(leave, out_shape=(jax.ShapeDtypeStruct((tok, width), bf16)...  1.07 us

profile of v4, /device:TPU:0, one launch (start us, length us, event | category | flops | bytes accessed | tf_op | source)
XLA Modules:
  0.0 33.9 jit_solution(10793191197072597067)
XLA Ops:
  0.6 32.2 %shard_map.59 = (bf16[128,4096]{1,0:T(8,128)(2,1)S(1)}, f32[128,512]{1,0:T(8,128)S(1)}) custom-call(bf16[128,4096]{1,0:T(8,128)(2,1)} %acts.1, bf16[128,512]{1,0:T(8,128)(2,1)} %go.1, s32[1024,512]{1,0:T(8,128)} %codes.1, f32[1,512]{1,0:T(1,128)} %bitcast.1), custom_call_target="tpu_custom_call" | custom-call | tf_op jit(solution)/shard_map/pallas_call | solution.py:326
  32.8 1.1 %shard_map.60 = (bf16[128,4096]{1,0:T(8,128)(2,1)}, f32[128,512]{1,0:T(8,128)}) custom-call(bf16[128,4096]{1,0:T(8,128)(2,1)S(1)} %get-tuple-element.4.gin, f32[128,512]{1,0:T(8,128)S(1)} %get-tuple-element.5.gw), custom_call_target="tpu_custom_call" | custom-call | tf_op jit(solution)/shard_map/pallas_call | solution.py:357

commit v5 on v4

--- a/solution.py
+++ b/solution.py
@@ -61,7 +61,8 @@
     mate = 2 * pair + 1 - lax.rem(z, 2)
     far_outer = 3 * (1 - pair)
     far_inner = 2 - pair
-    order = [far_outer, far_inner, mate, z]
+    swap = jnp.where(inner, mate - far_inner, 0)
+    order = [far_outer, far_inner + swap, mate - swap, z]
 
     def dev(ii, zz, cc):
         return {"intra": ii, "inter": 2 * zz + cc}
@@ -132,8 +133,10 @@
             part_go = go_half(me, 1 - n if late else n)
             send(part_go, part_go, go_send, go_recv.at[n, late], dev(peers[d], z, c))
 
+    pl.semaphore_signal(diag_sem, inc=1, device_id=dev(peers[near[0]], z, c), device_id_type=MESH)
     send_go(0)
-    pl.semaphore_signal(diag_sem, inc=1, device_id=dev(peers[near[0]], z, c), device_id_type=MESH)
+    send_go(1)
+    send(go_slot(me), go_slot(me), go_send, pair_recv.at[0], dev(i, z, oc))
 
     load_codes.wait()
     code_b[...] = codes_v[...].astype(jnp.float32).astype(jnp.bfloat16)
@@ -142,8 +145,6 @@
     send(scale_v, scale_d, s_send, s_recv, dev(dd, z, c))
     row_scale = lane_scale(scale_v[...], half)
     send(code_b.at[quarter(z)], code_d.at[quarter(z)], w_send.at[0], w_recv.at[z], dev(dd, z, c))
-    send_go(1)
-    send(go_slot(me), go_slot(me), go_send, pair_recv.at[0], dev(i, z, oc))
 
     load_acts.wait()
 
@@ -230,7 +231,6 @@
     @pl.when(inner)
     def _():
         landed(mate)
-        hop(1, mate, far_inner)
         hop(1, mate, far_outer)
         landed(far_inner)
         hop(1, far_inner, mate)
@@ -242,35 +242,54 @@
             ac[h], go_all[...], (((0,), (0,)), ((), ())), preferred_element_type=jnp.float32
         )
 
-    def pass_on(n, dst, recv, to):
-        send(part.at[n], dst, r_send, recv, dev(i, to, c))
-
-    def first_terms(n):
+    def rows_of(q):
+        return pl.ds(q * (blk // 2), blk // 2)
+
+    def pass_on(n, q, dst, recv, to):
+        send(part.at[n, rows_of(q)], dst.at[rows_of(q)], r_send, recv, dev(i, to, c))
+
+    def give(n, term, dst, recv):
+        part[n] = term.astype(jnp.bfloat16)
+        for q in range(2):
+            pass_on(n, q, dst, recv(q), mate)
+
+    def split(n, on_inner, on_outer):
         term = term_of(n)
-
-        @pl.when(inner)
-        def _():
+        pl.when(inner)(lambda: on_inner(term))
+        pl.when(jnp.logical_not(inner))(lambda: on_outer(term))
+
+    def hold(n):
+        def keep(term):
             held[n] = term
-
-        @pl.when(jnp.logical_not(inner))
-        def _():
-            part[n] = term.astype(jnp.bfloat16)
-            pass_on(n, ms.at[n], m_recv.at[n], mate)
-
-    def merge(n):
-        @pl.when(inner)
-        def _():
-            arrived(ms.at[n], m_recv.at[n])
-            part[n] = (held[n] + ms[n].astype(jnp.float32)).astype(jnp.bfloat16)
-            pass_on(n, rs.at[1], r_recv, order[n])
-
-    first_terms(0)
-    first_terms(1)
-
-    merge(0)
-    part[2] = term_of(2).astype(jnp.bfloat16)
-    pass_on(2, rs.at[0], r_recv, mate)
-    merge(1)
+        return keep
+
+    def to_merge(n):
+        return lambda term: give(n, term, ms.at[n], lambda q: m_recv.at[n, q])
+
+    def to_mate(term):
+        give(2, term, rs.at[0], lambda q: r_recv)
+
+    def merge(n, to):
+        for q in range(2):
+            arrived(ms.at[n, rows_of(q)], m_recv.at[n, q])
+            total = held[n, rows_of(q)] + ms[n, rows_of(q)].astype(jnp.float32)
+            part[n, rows_of(q)] = total.astype(jnp.bfloat16)
+            pass_on(n, q, rs.at[1], r_recv, to)
+
+    split(0, hold(0), to_merge(0))
+    split(1, to_mate, to_merge(1))
+
+    @pl.when(inner)
+    def _():
+        merge(0, far_outer)
+        hop(1, mate, far_inner)
+
+    split(2, hold(1), to_mate)
+
+    @pl.when(inner)
+    def _():
+        merge(1, far_inner)
+
     mine = term_of(3)
 
     @pl.when(jnp.logical_not(inner))
@@ -348,7 +367,7 @@
             dma((4,)),
             dma, dma((2, 2)), dma((ni,)), dma,
             dma, dma((nz,)), dma, dma,
-            dma, dma, dma((2,)),
+            dma, dma, dma((2, 2)),
             dma((2,)), dma((nz,)), dma, dma,
             *[pltpu.SemaphoreType.REGULAR] * 3,
         ],

time: 34 us -> 32.6 us (0.959)
  Pallas kernels: 33.2 us -> 31.7 us
    pallas_call x1, Pallas kernels: 32.2 us -> 30.6 us  [fused(): pl.pallas_call(functools.partial(kernel, ni, nj), out_shape=(pltpu.VMEM((...]
where the time goes in v5:
time: 32.6 us; the launch traced here: 32.3 us
  Pallas kernels  31.7 us (97%)
  between operations  0.64 us (2%)
    pallas_call x1, Pallas kernels, fused(): pl.pallas_call(functools.partial(kernel, ni, nj), out_shape=(pltpu.VMEM((...  30.6 us
    pallas_call x1, Pallas kernels, fused(): pl.pallas_call(leave, out_shape=(jax.ShapeDtypeStruct((tok, width), bf16)...  1.07 us

profile of v5, /device:TPU:0, one launch (start us, length us, event | category | flops | bytes accessed | tf_op | source)
XLA Modules:
  0.0 32.3 jit_solution(9281554891434713617)
XLA Ops:
  0.6 30.6 %shard_map.59 = (bf16[128,4096]{1,0:T(8,128)(2,1)S(1)}, f32[128,512]{1,0:T(8,128)S(1)}) custom-call(bf16[128,4096]{1,0:T(8,128)(2,1)} %acts.1, bf16[128,512]{1,0:T(8,128)(2,1)} %go.1, s32[1024,512]{1,0:T(8,128)} %codes.1, f32[1,512]{1,0:T(1,128)} %bitcast.1), custom_call_target="tpu_custom_call" | custom-call | tf_op jit(solution)/shard_map/pallas_call | solution.py:345
  31.3 1.1 %shard_map.60 = (bf16[128,4096]{1,0:T(8,128)(2,1)}, f32[128,512]{1,0:T(8,128)}) custom-call(bf16[128,4096]{1,0:T(8,128)(2,1)S(1)} %get-tuple-element.4.gin, f32[128,512]{1,0:T(8,128)S(1)} %get-tuple-element.5.gw), custom_call_target="tpu_custom_call" | custom-call | tf_op jit(solution)/shard_map/pallas_call | solution.py:376

commit v6 on v5

--- a/solution.py
+++ b/solution.py
@@ -93,8 +93,8 @@
     def cols_of(ii, cc):
         return pl.ds(pl.multiple_of(ii * rows + cc * half, half), half)
 
-    def quarter(h):
-        return pl.ds(pl.multiple_of(h * blk, blk), blk)
+    def quarter(h, q):
+        return pl.ds(pl.multiple_of(h * blk + q * (blk // 2), blk // 2), blk // 2)
 
     half_start = pl.multiple_of(c * half, half)
     sc_start = pl.multiple_of(c * (half // 2), half // 2)
@@ -144,7 +144,8 @@
     pl.semaphore_wait(diag_sem, 1)
     send(scale_v, scale_d, s_send, s_recv, dev(dd, z, c))
     row_scale = lane_scale(scale_v[...], half)
-    send(code_b.at[quarter(z)], code_d.at[quarter(z)], w_send.at[0], w_recv.at[z], dev(dd, z, c))
+    for q in range(2):
+        send(code_b.at[quarter(z, q)], code_d.at[quarter(z, q)], w_send.at[0], w_recv.at[z, q], dev(dd, z, c))
 
     load_acts.wait()
 
@@ -178,18 +179,19 @@
     def _():
         pl.semaphore_wait(line_sem, 1)
 
-    def hop(n, h, to):
-        send(code_d.at[quarter(h)], code_d.at[quarter(h)], w_send.at[n], w_recv.at[h], dev(i, to, c))
-
-    def landed(h):
-        arrived(code_d.at[quarter(h)], w_recv.at[h])
-
-    landed(z)
-    hop(0, z, mate)
-
-    @pl.when(inner)
-    def _():
-        hop(1, z, far_inner)
+    def hop(n, h, q, to):
+        send(code_d.at[quarter(h, q)], code_d.at[quarter(h, q)], w_send.at[n], w_recv.at[h, q], dev(i, to, c))
+
+    def landed(h, q):
+        arrived(code_d.at[quarter(h, q)], w_recv.at[h, q])
+
+    for q in range(2):
+        landed(z, q)
+        hop(0, z, q, mate)
+
+        @pl.when(inner)
+        def _():
+            hop(1, z, q, far_inner)
 
     for n, d in enumerate(near):
         m = 2 * peers[d] + c
@@ -230,10 +232,14 @@
 
     @pl.when(inner)
     def _():
-        landed(mate)
-        hop(1, mate, far_outer)
-        landed(far_inner)
-        hop(1, far_inner, mate)
+        for q in range(2):
+            landed(mate, q)
+            hop(1, mate, q, far_outer)
+        for q in range(2):
+            hop(1, mate, q, far_inner)
+        for q in range(2):
+            landed(far_inner, q)
+            hop(1, far_inner, q, mate)
 
     def term_of(n):
         h = order[n]
@@ -282,7 +288,6 @@
     @pl.when(inner)
     def _():
         merge(0, far_outer)
-        hop(1, mate, far_inner)
 
     split(2, hold(1), to_mate)
 
@@ -294,10 +299,12 @@
 
     @pl.when(jnp.logical_not(inner))
     def _():
-        landed(mate)
-        landed(far_inner)
-
-    landed(far_outer)
+        for q in range(2):
+            landed(mate, q)
+            landed(far_inner, q)
+
+    for q in range(2):
+        landed(far_outer, q)
 
     pieces[diag] = pieces_of(i, code_d, far_scale)
     own_piece(diag, dd)
@@ -368,7 +375,7 @@
             dma, dma((2, 2)), dma((ni,)), dma,
             dma, dma((nz,)), dma, dma,
             dma, dma, dma((2, 2)),
-            dma((2,)), dma((nz,)), dma, dma,
+            dma((2,)), dma((nz, 2)), dma, dma,
             *[pltpu.SemaphoreType.REGULAR] * 3,
         ],
         compiler_params=pltpu.CompilerParams(collective_id=0, has_side_effects=True),

time: 32.6 us -> 32.1 us (0.985)
  Pallas kernels: 31.7 us -> 31.3 us
    pallas_call x1, Pallas kernels: 30.6 us -> 30.2 us  [fused(): pl.pallas_call(functools.partial(kernel, ni, nj), out_shape=(pltpu.VMEM((...]
where the time goes in v6:
time: 32.1 us; the launch traced here: 31.9 us
  Pallas kernels  31.3 us (98%)
  between operations  0.64 us (2%)
    pallas_call x1, Pallas kernels, fused(): pl.pallas_call(functools.partial(kernel, ni, nj), out_shape=(pltpu.VMEM((...  30.2 us
    pallas_call x1, Pallas kernels, fused(): pl.pallas_call(leave, out_shape=(jax.ShapeDtypeStruct((tok, width), bf16)...  1.07 us

profile of v6, /device:TPU:0, one launch (start us, length us, event | category | flops | bytes accessed | tf_op | source)
XLA Modules:
  0.0 31.9 jit_solution(17616099940680033272)
XLA Ops:
  0.6 30.2 %shard_map.59 = (bf16[128,4096]{1,0:T(8,128)(2,1)S(1)}, f32[128,512]{1,0:T(8,128)S(1)}) custom-call(bf16[128,4096]{1,0:T(8,128)(2,1)} %acts.1, bf16[128,512]{1,0:T(8,128)(2,1)} %go.1, s32[1024,512]{1,0:T(8,128)} %codes.1, f32[1,512]{1,0:T(1,128)} %bitcast.1), custom_call_target="tpu_custom_call" | custom-call | tf_op jit(solution)/shard_map/pallas_call | solution.py:352
  30.8 1.1 %shard_map.60 = (bf16[128,4096]{1,0:T(8,128)(2,1)}, f32[128,512]{1,0:T(8,128)}) custom-call(bf16[128,4096]{1,0:T(8,128)(2,1)S(1)} %get-tuple-element.4.gin, f32[128,512]{1,0:T(8,128)S(1)} %get-tuple-element.5.gw), custom_call_target="tpu_custom_call" | custom-call | tf_op jit(solution)/shard_map/pallas_call | solution.py:383

commit v7 on v6

--- a/solution.py
+++ b/solution.py
@@ -93,8 +93,16 @@
     def cols_of(ii, cc):
         return pl.ds(pl.multiple_of(ii * rows + cc * half, half), half)
 
-    def quarter(h, q):
-        return pl.ds(pl.multiple_of(h * blk + q * (blk // 2), blk // 2), blk // 2)
+    less = blk * 3 // 4
+    share = {False: less, True: 2 * blk - less}
+
+    def shares(h, q, big):
+        start = (h // 2) * (2 * blk) + lax.rem(h, 2) * share[not big] + q * (share[big] // 2)
+        return pl.ds(pl.multiple_of(start, 16), share[big] // 2)
+
+    def by_kind(work):
+        pl.when(inner)(lambda: work(True))
+        pl.when(jnp.logical_not(inner))(lambda: work(False))
 
     half_start = pl.multiple_of(c * half, half)
     sc_start = pl.multiple_of(c * (half // 2), half // 2)
@@ -144,8 +152,13 @@
     pl.semaphore_wait(diag_sem, 1)
     send(scale_v, scale_d, s_send, s_recv, dev(dd, z, c))
     row_scale = lane_scale(scale_v[...], half)
-    for q in range(2):
-        send(code_b.at[quarter(z, q)], code_d.at[quarter(z, q)], w_send.at[0], w_recv.at[z, q], dev(dd, z, c))
+
+    @by_kind
+    def _(big):
+        for q in range(2):
+            rows_q = shares(z, q, big)
+            send(code_b.at[rows_q], code_d.at[rows_q], w_send.at[0], w_recv.at[z, q], dev(dd, z, c))
+
 
     load_acts.wait()
 
@@ -179,19 +192,20 @@
     def _():
         pl.semaphore_wait(line_sem, 1)
 
-    def hop(n, h, q, to):
-        send(code_d.at[quarter(h, q)], code_d.at[quarter(h, q)], w_send.at[n], w_recv.at[h, q], dev(i, to, c))
-
-    def landed(h, q):
-        arrived(code_d.at[quarter(h, q)], w_recv.at[h, q])
-
-    for q in range(2):
-        landed(z, q)
-        hop(0, z, q, mate)
-
-        @pl.when(inner)
-        def _():
-            hop(1, z, q, far_inner)
+    def hop(n, h, q, big, to):
+        rows_q = code_d.at[shares(h, q, big)]
+        send(rows_q, rows_q, w_send.at[n], w_recv.at[h, q], dev(i, to, c))
+
+    def landed(h, q, big):
+        arrived(code_d.at[shares(h, q, big)], w_recv.at[h, q])
+
+    @by_kind
+    def _(big):
+        for q in range(2):
+            landed(z, q, big)
+            hop(0, z, q, big, mate)
+            if big:
+                hop(1, z, q, big, far_inner)
 
     for n, d in enumerate(near):
         m = 2 * peers[d] + c
@@ -233,13 +247,13 @@
     @pl.when(inner)
     def _():
         for q in range(2):
-            landed(mate, q)
-            hop(1, mate, q, far_outer)
-        for q in range(2):
-            hop(1, mate, q, far_inner)
-        for q in range(2):
-            landed(far_inner, q)
-            hop(1, far_inner, q, mate)
+            landed(mate, q, False)
+            hop(1, mate, q, False, far_outer)
+        for q in range(2):
+            hop(1, mate, q, False, far_inner)
+        for q in range(2):
+            landed(far_inner, q, True)
+            hop(1, far_inner, q, True, mate)
 
     def term_of(n):
         h = order[n]
@@ -300,11 +314,11 @@
     @pl.when(jnp.logical_not(inner))
     def _():
         for q in range(2):
-            landed(mate, q)
-            landed(far_inner, q)
+            landed(mate, q, True)
+            landed(far_inner, q, True)
 
     for q in range(2):
-        landed(far_outer, q)
+        landed(far_outer, q, False)
 
     pieces[diag] = pieces_of(i, code_d, far_scale)
     own_piece(diag, dd)
@@ -317,12 +331,13 @@
     drained(go_all.at[pl.ds(0, (2 * ni - 1) * tok)], go_send)
     drained(acts_v.at[:, pl.ds(0, nz * (2 * ni - 1) * blk)], a_send)
     drained(part, r_send)
-    drained(code_d.at[pl.ds(0, 2 * blk)], w_send.at[0])
     drained(scale_v, s_send)
 
-    @pl.when(inner)
-    def _():
-        drained(code_d, w_send.at[1])
+    @by_kind
+    def _(big):
+        drained(code_d.at[pl.ds(0, 2 * share[big])], w_send.at[0])
+        if big:
+            drained(code_d, w_send.at[1])
 
     pieces_all = gin.at[:, pl.ds(0, 6 * half)]
     drained(pieces_all, p_send)

time: 32.1 us -> 31.7 us (0.988)
  Pallas kernels: 31.3 us -> 30.9 us
    pallas_call x1, Pallas kernels: 30.2 us -> 29.8 us  [fused(): pl.pallas_call(functools.partial(kernel, ni, nj), out_shape=(pltpu.VMEM((...]
where the time goes in v7:
time: 31.7 us; the launch traced here: 31.5 us
  Pallas kernels  30.9 us (97%)
  between operations  0.64 us (2%)
    pallas_call x1, Pallas kernels, fused(): pl.pallas_call(functools.partial(kernel, ni, nj), out_shape=(pltpu.VMEM((...  29.8 us
    pallas_call x1, Pallas kernels, fused(): pl.pallas_call(leave, out_shape=(jax.ShapeDtypeStruct((tok, width), bf16)...  1.07 us

profile of v7, /device:TPU:0, one launch (start us, length us, event | category | flops | bytes accessed | tf_op | source)
XLA Modules:
  0.0 31.5 jit_solution(8980884218642261102)
XLA Ops:
  0.6 29.8 %shard_map.59 = (bf16[128,4096]{1,0:T(8,128)(2,1)S(1)}, f32[128,512]{1,0:T(8,128)S(1)}) custom-call(bf16[128,4096]{1,0:T(8,128)(2,1)} %acts.1, bf16[128,512]{1,0:T(8,128)(2,1)} %go.1, s32[1024,512]{1,0:T(8,128)} %codes.1, f32[1,512]{1,0:T(1,128)} %bitcast.1), custom_call_target="tpu_custom_call" | custom-call | tf_op jit(solution)/shard_map/pallas_call | solution.py:367
  30.5 1.1 %shard_map.60 = (bf16[128,4096]{1,0:T(8,128)(2,1)}, f32[128,512]{1,0:T(8,128)}) custom-call(bf16[128,4096]{1,0:T(8,128)(2,1)S(1)} %get-tuple-element.4.gin, f32[128,512]{1,0:T(8,128)S(1)} %get-tuple-element.5.gw), custom_call_target="tpu_custom_call" | custom-call | tf_op jit(solution)/shard_map/pallas_call | solution.py:398

commit v8 on v5

--- a/solution.py
+++ b/solution.py
@@ -93,8 +93,15 @@
     def cols_of(ii, cc):
         return pl.ds(pl.multiple_of(ii * rows + cc * half, half), half)
 
-    def quarter(h):
-        return pl.ds(pl.multiple_of(h * blk, blk), blk)
+    share = [blk * n // 8 for n in (6, 9, 10, 7)]
+
+    def shares(h, q):
+        early = (share[h] // 2 + 15) // 16 * 16
+        return pl.ds(sum(share[:h]) + q * early, share[h] - early if q else early)
+
+    def by_plane(work):
+        for k in range(nz):
+            pl.when(z == k)(functools.partial(work, k))
 
     half_start = pl.multiple_of(c * half, half)
     sc_start = pl.multiple_of(c * (half // 2), half // 2)
@@ -144,7 +151,13 @@
     pl.semaphore_wait(diag_sem, 1)
     send(scale_v, scale_d, s_send, s_recv, dev(dd, z, c))
     row_scale = lane_scale(scale_v[...], half)
-    send(code_b.at[quarter(z)], code_d.at[quarter(z)], w_send.at[0], w_recv.at[z], dev(dd, z, c))
+
+    @by_plane
+    def _(k):
+        for q in range(2):
+            rows_q = shares(k, q)
+            send(code_b.at[rows_q], code_d.at[rows_q], w_send.at[0], w_recv.at[k, q], dev(dd, z, c))
+
 
     load_acts.wait()
 
@@ -178,18 +191,20 @@
     def _():
         pl.semaphore_wait(line_sem, 1)
 
-    def hop(n, h, to):
-        send(code_d.at[quarter(h)], code_d.at[quarter(h)], w_send.at[n], w_recv.at[h], dev(i, to, c))
-
-    def landed(h):
-        arrived(code_d.at[quarter(h)], w_recv.at[h])
-
-    landed(z)
-    hop(0, z, mate)
-
-    @pl.when(inner)
-    def _():
-        hop(1, z, far_inner)
+    def hop(n, h, q, to):
+        rows_q = code_d.at[shares(h, q)]
+        send(rows_q, rows_q, w_send.at[n], w_recv.at[h, q], dev(i, to, c))
+
+    def landed(h, q):
+        arrived(code_d.at[shares(h, q)], w_recv.at[h, q])
+
+    @by_plane
+    def _(k):
+        for q in range(2):
+            landed(k, q)
+            hop(0, k, q, k ^ 1)
+            if k in (1, 2):
+                hop(1, k, q, 3 - k)
 
     for n, d in enumerate(near):
         m = 2 * peers[d] + c
@@ -214,26 +229,18 @@
         gin[:, cols_of(ii, c)] = piece(n, c)[...]
         send(piece(n, oc), gin.at[:, cols_of(ii, c)], p_send, p_recv, dev(i, z, oc))
 
-    for d in near:
-        ii = peers[d]
-        wait_pair(d)
-        pieces[d] = pieces_of(ii, code_b, row_scale)
-        for cc in cores:
-            send(piece(d, cc), gin.at[:, cols_of(i, c)], p_send, p_recv, dev(ii, z, cc))
-    wait_pair(0)
-    pieces[0] = pieces_of(i, code_b, row_scale)
-    own_piece(0, i)
-
-    arrived(scale_d, s_recv)
-    far_scale = lane_scale(scale_d[...], half)
-    wait_pair(diag)
-
-    @pl.when(inner)
-    def _():
-        landed(mate)
-        hop(1, mate, far_outer)
-        landed(far_inner)
-        hop(1, far_inner, mate)
+
+    @by_plane
+    def _(k):
+        if k in (1, 2):
+            for q in range(2):
+                landed(k ^ 1, q)
+                hop(1, k ^ 1, q, (3 - k) ^ 1)
+            for q in range(2):
+                hop(1, k ^ 1, q, 3 - k)
+            for q in range(2):
+                landed(3 - k, q)
+                hop(2, 3 - k, q, k ^ 1)
 
     def term_of(n):
         h = order[n]
@@ -276,13 +283,23 @@
             part[n, rows_of(q)] = total.astype(jnp.bfloat16)
             pass_on(n, q, rs.at[1], r_recv, to)
 
+    for d in range(ni):
+        wait_pair(d)
     split(0, hold(0), to_merge(0))
+
+    for d in near:
+        ii = peers[d]
+        pieces[d] = pieces_of(ii, code_b, row_scale)
+        for cc in cores:
+            send(piece(d, cc), gin.at[:, cols_of(i, c)], p_send, p_recv, dev(ii, z, cc))
+    pieces[0] = pieces_of(i, code_b, row_scale)
+    own_piece(0, i)
+
     split(1, to_mate, to_merge(1))
 
     @pl.when(inner)
     def _():
         merge(0, far_outer)
-        hop(1, mate, far_inner)
 
     split(2, hold(1), to_mate)
 
@@ -292,14 +309,15 @@
 
     mine = term_of(3)
 
-    @pl.when(jnp.logical_not(inner))
-    def _():
-        landed(mate)
-        landed(far_inner)
-
-    landed(far_outer)
-
-    pieces[diag] = pieces_of(i, code_d, far_scale)
+    @by_plane
+    def _(k):
+        left = ((3 - k) ^ 1,) if k in (1, 2) else (k ^ 1, (3 - k) ^ 1, 3 - k)
+        for h in left:
+            for q in range(2):
+                landed(h, q)
+
+    arrived(scale_d, s_recv)
+    pieces[diag] = pieces_of(i, code_d, lane_scale(scale_d[...], half))
     own_piece(diag, dd)
 
     arrived(rs, r_recv)
@@ -310,12 +328,14 @@
     drained(go_all.at[pl.ds(0, (2 * ni - 1) * tok)], go_send)
     drained(acts_v.at[:, pl.ds(0, nz * (2 * ni - 1) * blk)], a_send)
     drained(part, r_send)
-    drained(code_d.at[pl.ds(0, 2 * blk)], w_send.at[0])
     drained(scale_v, s_send)
 
-    @pl.when(inner)
-    def _():
-        drained(code_d, w_send.at[1])
+    @by_plane
+    def _(k):
+        drained(code_d.at[pl.ds(0, 2 * share[k])], w_send.at[0])
+        if k in (1, 2):
+            drained(code_d.at[pl.ds(0, share[k] + 2 * share[k ^ 1])], w_send.at[1])
+            drained(code_d.at[pl.ds(0, share[3 - k])], w_send.at[2])
 
     pieces_all = gin.at[:, pl.ds(0, 6 * half)]
     drained(pieces_all, p_send)
@@ -368,7 +388,7 @@
             dma, dma((2, 2)), dma((ni,)), dma,
             dma, dma((nz,)), dma, dma,
             dma, dma, dma((2, 2)),
-            dma((2,)), dma((nz,)), dma, dma,
+            dma((3,)), dma((nz, 2)), dma, dma,
             *[pltpu.SemaphoreType.REGULAR] * 3,
         ],
         compiler_params=pltpu.CompilerParams(collective_id=0, has_side_effects=True),

time: 32.6 us -> 31.6 us (0.969)
  Pallas kernels: 31.7 us -> 30.6 us
    pallas_call x1, Pallas kernels: 30.6 us -> 29.5 us  [fused(): pl.pallas_call(functools.partial(kernel, ni, nj), out_shape=(pltpu.VMEM((...]
where the time goes in v8:
time: 31.6 us; the launch traced here: 31.2 us
  Pallas kernels  30.6 us (97%)
  between operations  0.64 us (2%)
    pallas_call x1, Pallas kernels, fused(): pl.pallas_call(functools.partial(kernel, ni, nj), out_shape=(pltpu.VMEM((...  29.5 us
    pallas_call x1, Pallas kernels, fused(): pl.pallas_call(leave, out_shape=(jax.ShapeDtypeStruct((tok, width), bf16)...  1.07 us

profile of v8, /device:TPU:0, one launch (start us, length us, event | category | flops | bytes accessed | tf_op | source)
XLA Modules:
  0.0 31.2 jit_solution(7716848032825236013)
XLA Ops:
  0.6 29.5 %shard_map.59 = (bf16[128,4096]{1,0:T(8,128)(2,1)S(1)}, f32[128,512]{1,0:T(8,128)S(1)}) custom-call(bf16[128,4096]{1,0:T(8,128)(2,1)} %acts.1, bf16[128,512]{1,0:T(8,128)(2,1)} %go.1, s32[1024,512]{1,0:T(8,128)} %codes.1, f32[1,512]{1,0:T(1,128)} %bitcast.1), custom_call_target="tpu_custom_call" | custom-call | tf_op jit(solution)/shard_map/pallas_call | solution.py:365
  30.2 1.1 %shard_map.60 = (bf16[128,4096]{1,0:T(8,128)(2,1)}, f32[128,512]{1,0:T(8,128)}) custom-call(bf16[128,4096]{1,0:T(8,128)(2,1)S(1)} %get-tuple-element.4.gin, f32[128,512]{1,0:T(8,128)S(1)} %get-tuple-element.5.gw), custom_call_target="tpu_custom_call" | custom-call | tf_op jit(solution)/shard_map/pallas_call | solution.py:396

commit v9 on v8

--- a/solution.py
+++ b/solution.py
@@ -107,11 +107,11 @@
     sc_start = pl.multiple_of(c * (half // 2), half // 2)
     barrier = pltpu.get_barrier_semaphore()
     for d in near:
-        pl.semaphore_signal(barrier, inc=1, device_id=dev(peers[d], z, 0), device_id_type=MESH)
-
-    @pl.when(c == 1)
-    def _():
-        pl.semaphore_signal(barrier, inc=1, device_id=dev(i, z, 0), device_id_type=MESH)
+        pl.semaphore_signal(barrier, inc=1, device_id=dev(peers[d], z, 1), device_id_type=MESH)
+
+    @pl.when(c == 0)
+    def _():
+        pl.semaphore_signal(barrier, inc=1, device_id=dev(i, z, 1), device_id_type=MESH)
 
     load_go = pltpu.make_async_copy(go, go_slot(me), load_sem.at[0])
     load_go.start()
@@ -122,16 +122,16 @@
     load_scale = pltpu.make_async_copy(scales.at[:, pl.ds(sc_start, half // 2)], scale_v, load_sem.at[3])
     load_scale.start()
     for k in range(1, nz):
-        pl.semaphore_signal(barrier, inc=1, device_id=dev(i, lax.rem(z + k, nz), 1), device_id_type=MESH)
+        pl.semaphore_signal(barrier, inc=1, device_id=dev(i, lax.rem(z + k, nz), 0), device_id_type=MESH)
 
     load_go.wait()
 
+    @pl.when(c == 1)
+    def _():
+        pl.semaphore_wait(barrier, 2 * len(near) + 1)
+        pl.semaphore_signal(near_sem, inc=1, device_id=dev(i, z, 0), device_id_type=MESH)
+
     @pl.when(c == 0)
-    def _():
-        pl.semaphore_wait(barrier, 2 * len(near) + 1)
-        pl.semaphore_signal(near_sem, inc=1, device_id=dev(i, z, 1), device_id_type=MESH)
-
-    @pl.when(c == 1)
     def _():
         pl.semaphore_wait(near_sem, 1)
 
@@ -182,12 +182,12 @@
     for n in range(nz):
         send_columns(n)
 
+    @pl.when(c == 0)
+    def _():
+        pl.semaphore_wait(barrier, 2 * (nz - 1))
+        pl.semaphore_signal(line_sem, inc=1, device_id=dev(i, z, 1), device_id_type=MESH)
+
     @pl.when(c == 1)
-    def _():
-        pl.semaphore_wait(barrier, 2 * (nz - 1))
-        pl.semaphore_signal(line_sem, inc=1, device_id=dev(i, z, 0), device_id_type=MESH)
-
-    @pl.when(c == 0)
     def _():
         pl.semaphore_wait(line_sem, 1)
 

time: 31.6 us -> 30.9 us (0.978)
  the two profiles are of different devices: /device:TPU:0 before, /device:TPU:17 now
where the time goes in v9:
time: 30.9 us; the launch traced here: 30.8 us
  Pallas kernels  30.1 us (97%)
  between operations  0.64 us (2%)
    pallas_call x1, Pallas kernels, fused(): pl.pallas_call(functools.partial(kernel, ni, nj), out_shape=(pltpu.VMEM((...  29.1 us
    pallas_call x1, Pallas kernels, fused(): pl.pallas_call(leave, out_shape=(jax.ShapeDtypeStruct((tok, width), bf16)...  1.07 us

profile of v9, /device:TPU:17, one launch (start us, length us, event | category | flops | bytes accessed | tf_op | source)
XLA Modules:
  0.0 30.8 jit_solution(6893583922333608099)
XLA Ops:
  0.6 29.1 %shard_map.59 = (bf16[128,4096]{1,0:T(8,128)(2,1)S(1)}, f32[128,512]{1,0:T(8,128)S(1)}) custom-call(bf16[128,4096]{1,0:T(8,128)(2,1)} %acts.1, bf16[128,512]{1,0:T(8,128)(2,1)} %go.1, s32[1024,512]{1,0:T(8,128)} %codes.1, f32[1,512]{1,0:T(1,128)} %bitcast.1), custom_call_target="tpu_custom_call" | custom-call | tf_op jit(solution)/shard_map/pallas_call | solution.py:365
  29.7 1.1 %shard_map.60 = (bf16[128,4096]{1,0:T(8,128)(2,1)}, f32[128,512]{1,0:T(8,128)}) custom-call(bf16[128,4096]{1,0:T(8,128)(2,1)S(1)} %get-tuple-element.4.gin, f32[128,512]{1,0:T(8,128)S(1)} %get-tuple-element.5.gw), custom_call_target="tpu_custom_call" | custom-call | tf_op jit(solution)/shard_map/pallas_call | solution.py:396

commit v10 on v9

--- a/solution.py
+++ b/solution.py
@@ -93,7 +93,7 @@
     def cols_of(ii, cc):
         return pl.ds(pl.multiple_of(ii * rows + cc * half, half), half)
 
-    share = [blk * n // 8 for n in (6, 9, 10, 7)]
+    share = [blk * n // 8 for n in (7, 9, 9, 7)]
 
     def shares(h, q):
         early = (share[h] // 2 + 15) // 16 * 16

time: 30.9 us -> 30.7 us (level)
  the two profiles are of different devices: /device:TPU:17 before, /device:TPU:0 now
where the time goes in v10:
time: 30.7 us; the launch traced here: 30.5 us
  Pallas kernels  29.9 us (97%)
  between operations  0.64 us (2%)
    pallas_call x1, Pallas kernels, fused(): pl.pallas_call(functools.partial(kernel, ni, nj), out_shape=(pltpu.VMEM((...  28.8 us
    pallas_call x1, Pallas kernels, fused(): pl.pallas_call(leave, out_shape=(jax.ShapeDtypeStruct((tok, width), bf16)...  1.07 us

profile of v10, /device:TPU:0, one launch (start us, length us, event | category | flops | bytes accessed | tf_op | source)
XLA Modules:
  0.0 30.5 jit_solution(3633134971811546222)
XLA Ops:
  0.6 28.8 %shard_map.59 = (bf16[128,4096]{1,0:T(8,128)(2,1)S(1)}, f32[128,512]{1,0:T(8,128)S(1)}) custom-call(bf16[128,4096]{1,0:T(8,128)(2,1)} %acts.1, bf16[128,512]{1,0:T(8,128)(2,1)} %go.1, s32[1024,512]{1,0:T(8,128)} %codes.1, f32[1,512]{1,0:T(1,128)} %bitcast.1), custom_call_target="tpu_custom_call" | custom-call | tf_op jit(solution)/shard_map/pallas_call | solution.py:365
  29.4 1.1 %shard_map.60 = (bf16[128,4096]{1,0:T(8,128)(2,1)}, f32[128,512]{1,0:T(8,128)}) custom-call(bf16[128,4096]{1,0:T(8,128)(2,1)S(1)} %get-tuple-element.4.gin, f32[128,512]{1,0:T(8,128)S(1)} %get-tuple-element.5.gw), custom_call_target="tpu_custom_call" | custom-call | tf_op jit(solution)/shard_map/pallas_call | solution.py:396
